TPU v7x, 32 devices: a whole 2x2x4 slice. The times are simulated.
32 devices in a mesh: tm: 16 (over z, x, core), tile: 2 (over y).
Axes of the slice: x: 2, y: 2, z: 4, core: 2. Of those that a mesh axis runs over, the one named last changes fastest.
Arguments:
- queries: bfloat16 [32, 4, 64, 2560], P('tm', 'tile'), may hold values from -40 to 40
- keys: bfloat16 [32, 4, 64, 2560], P('tm', 'tile'), may hold values from -6 to 6
- values: bfloat16 [32, 4, 64, 2560], P('tm', 'tile'), may hold values from -6 to 6
- neighbours: int32 [16, 2, 3], P('tm', 'tile'), may hold values from -1 to 14, as said below
- halo_rows: int32 [16, 2], P('tm', 'tile'), may hold values from 0 to 2, as said below
Outputs:
- attended: bfloat16 [32, 4, 64, 2560], P('tm', 'tile')
Inputs may be any that keep to these rules, and one draw needn't show every extreme that they name: `neighbours`: for frame block b and tile t, the entries that are not -1 are distinct frame blocks from max(0, b - 5) to b - 1; lists hold 0 to 3 entries, and some list is full. `halo_rows`: some frame block and tile reads 2 rows.
All inputs are finite; a program needn't handle non-finite values.
Results may differ from a plain program's by a relative error of at most 0.0046.
Values may be sent and summed in bfloat16 or wider, within the bound.
A program may use at most 128 MiB of HBM per device.

v0:
```python
import math

import jax
import jax.numpy as jnp
from jax import lax
from jax.sharding import PartitionSpec as P

HD = 128
HMAX = 2
WIN = 5


def padded_2(x, sides, width):
    for axis, dim in sides:
        size, length = (lax.axis_size(axis), x.shape[dim])
        up = [(i, (i + 1) % size) for i in range(size - 1)]
        down = [(j, i) for i, j in up]
        last = lax.slice_in_dim(x, length - width, length, axis=dim)
        leading = lax.slice_in_dim(x, 0, width, axis=dim)
        before = lax.ppermute(last, axis, up)
        after = lax.ppermute(leading, axis, down)
        x = jnp.concatenate([before, x, after], axis=dim)
    return x


def from_behind(value, axis, steps):
    count = lax.axis_size(axis)
    leading, last = (max(0, -steps), min(count, count - steps))
    return lax.ppermute(value, axis, [(source, source + steps) for source in range(leading, last)])


def head_groups(query_rows, key_rows, value_rows, allowed):
    tokens, channels = query_rows.shape
    head_count = channels // HD
    key_count = key_rows.shape[0]
    group_size = 2
    group_count = head_count // group_size
    columns = group_size * HD

    def one_group(group_index):
        offset = group_index * columns
        query_part = lax.dynamic_slice_in_dim(query_rows, offset, columns, 1).reshape(
            tokens, group_size, HD
        )
        key_part = lax.dynamic_slice_in_dim(key_rows, offset, columns, 1).reshape(
            key_count, group_size, HD
        )
        value_part = lax.dynamic_slice_in_dim(value_rows, offset, columns, 1).reshape(
            key_count, group_size, HD
        )
        scores = jnp.einsum(
            "qhd,khd->hqk", query_part, key_part, preferred_element_type=jnp.float32
        ) / math.sqrt(HD)
        scores = jnp.where(allowed[None], scores, -jnp.inf)
        maximum = jnp.max(scores, axis=2, keepdims=True)
        weights = jnp.where(allowed[None], jnp.exp(scores - maximum), 0.0)
        totals = jnp.sum(weights, axis=2)
        numerator = jnp.einsum(
            "hqk,khd->qhd",
            weights.astype(jnp.bfloat16),
            value_part,
            preferred_element_type=jnp.float32,
        )
        return (numerator / totals.T[:, :, None]).reshape(tokens, columns).astype(jnp.bfloat16)

    pieces = lax.map(one_group, jnp.arange(group_count, dtype=jnp.int32))
    return pieces.transpose(1, 0, 2).reshape(tokens, channels)


def local(queries, keys, values, neighbours, halo_rows):
    frames, tile_rows, grid_columns, channels = queries.shape
    tokens = frames * tile_rows * grid_columns
    span_rows = tile_rows + 2 * HMAX
    block_index = lax.axis_index("tm")
    tile_index = lax.axis_index("tile")
    tile_count = lax.axis_size("tile")
    key_value = jnp.stack((keys, values))
    padded = padded_2(key_value, (("tile", 2),), HMAX)
    moving = key_value
    earlier = []
    for hop_number in range(WIN):
        moving = from_behind(moving, "tm", 1)
        earlier.append(moving)
    stacked = jnp.stack(earlier)
    listed = neighbours[0, 0]
    halo_reach = halo_rows[0, 0]
    position = jnp.clip(block_index - listed - 1, 0, WIN - 1)
    chosen = jnp.take(stacked, position, axis=0)
    present = listed >= 0
    query_frame = lax.broadcasted_iota(jnp.int32, (frames, tile_rows, grid_columns), 0).reshape(-1)
    key_frame = lax.broadcasted_iota(jnp.int32, (frames, span_rows, grid_columns), 0).reshape(-1)
    key_row = lax.broadcasted_iota(jnp.int32, (frames, span_rows, grid_columns), 1).reshape(-1)
    global_row = tile_index * tile_rows - HMAX + key_row
    row_ok = (
        (global_row >= 0)
        & (global_row < tile_rows * tile_count)
        & (key_row >= HMAX - halo_reach)
        & (key_row < HMAX + tile_rows + halo_reach)
    )
    own_mask = (key_frame[None, :] <= query_frame[:, None]) & row_ok[None, :]
    slot_mask = jnp.repeat(present, tokens)
    allowed = jnp.concatenate(
        (own_mask, jnp.broadcast_to(slot_mask[None, :], (tokens, slot_mask.shape[0]))), axis=1
    )
    key_rows = jnp.concatenate(
        (padded[0].reshape(-1, channels), chosen[:, 0].reshape(-1, channels)), axis=0
    )
    value_rows = jnp.concatenate(
        (padded[1].reshape(-1, channels), chosen[:, 1].reshape(-1, channels)), axis=0
    )
    result = head_groups(queries.reshape(tokens, channels), key_rows, value_rows, allowed)
    return result.reshape(frames, tile_rows, grid_columns, channels)


def solution(mesh):
    return jax.shard_map(
        local,
        mesh=mesh,
        in_specs=(
            P("tm", "tile", None, None),
            P("tm", "tile", None, None),
            P("tm", "tile", None, None),
            P("tm", "tile", None),
            P("tm", "tile"),
        ),
        out_specs=P("tm", "tile", None, None),
        check_vma=False,
    )
```

profile of v0, /device:TPU:16, one launch (start us, length us, event | category | flops | bytes accessed | tf_op | source)
XLA Modules:
  0.0 332.4 jit_solution(14864586410358250011)
XLA Ops:
  0.0 3.6 %pad_maximum_fusion.3 = bf16[2,2,2,64,2560]{4,3,2,1,0:T(8,128)(2,1)} fusion(bf16[1,2,2,64,2560]{4,3,2,1,0:T(8,128)(2,1)} %bitcast.76, bf16[1,2,2,64,2560]{4,3,2,1,0:T(8,128)(2,1)} %bitcast.78), kind=kLoop, calls=%fused_computation.27 | loop fusion | flops 1310720 | bytes 5242880 | tf_op jit(solution)/shard_map/stack | solution.py:77
  3.6 1.9 collective-permute-start.2
  5.5 32.2 %collective-permute-done.2 = bf16[2,2,2,64,2560]{4,3,2,1,0:T(8,128)(2,1)S(1)} collective-permute-done((bf16[2,2,2,64,2560]{4,3,2,1,0:T(8,128)(2,1)}, bf16[2,2,2,64,2560]{4,3,2,1,0:T(8,128)(2,1)S(1)}, u32[]{:S(2)}, u32[]{:S(2)}) %collective-permute-start.2) | collective-permute-done | bytes 2621472 | tf_op jit(solution)/shard_map/ppermute | solution.py:29
  39.2 1.9 collective-permute-start.3
  41.1 32.0 %collective-permute-done.3 = bf16[2,2,2,64,2560]{4,3,2,1,0:T(8,128)(2,1)} collective-permute-done((bf16[2,2,2,64,2560]{4,3,2,1,0:T(8,128)(2,1)S(1)}, bf16[2,2,2,64,2560]{4,3,2,1,0:T(8,128)(2,1)}, u32[]{:S(2)}, u32[]{:S(2)}) %collective-permute-start.3) | collective-permute-done | bytes 2621472 | tf_op jit(solution)/shard_map/ppermute | solution.py:29
  73.2 1.9 collective-permute-start.4
  75.1 5.0 %collective-permute-start = (bf16[2,2,2,64,2560]{4,3,2,1,0:T(8,128)(2,1)}, bf16[2,2,2,64,2560]{4,3,2,1,0:T(8,128)(2,1)}, u32[]{:S(2)}, u32[]{:S(2)}) collective-permute-start(bf16[2,2,2,64,2560]{4,3,2,1,0:T(8,128)(2,1)} %pad_maximum_fusion.3), channel_id=1, source_target_pairs={{0,1},{2,3},{4,5},{6,7},{8,9},{10,11},{12,13},{14,15},{16,17},{18,... | collective-permute-start | bytes 7864328 | tf_op jit(solution)/shard_map/ppermute | solution.py:20
  82.1 25.3 %collective-permute-done.4 = bf16[2,2,2,64,2560]{4,3,2,1,0:T(8,128)(2,1)} collective-permute-done((bf16[2,2,2,64,2560]{4,3,2,1,0:T(8,128)(2,1)}, bf16[2,2,2,64,2560]{4,3,2,1,0:T(8,128)(2,1)}, u32[]{:S(2)}, u32[]{:S(2)}) %collective-permute-start.4) | collective-permute-done | bytes 2621472 | tf_op jit(solution)/shard_map/ppermute | solution.py:29
  107.4 1.9 collective-permute-start.5
  110.0 24.9 %collective-permute-done = bf16[2,2,2,64,2560]{4,3,2,1,0:T(8,128)(2,1)} collective-permute-done((bf16[2,2,2,64,2560]{4,3,2,1,0:T(8,128)(2,1)}, bf16[2,2,2,64,2560]{4,3,2,1,0:T(8,128)(2,1)}, u32[]{:S(2)}, u32[]{:S(2)}) %collective-permute-start) | collective-permute-done | bytes 2621472 | tf_op jit(solution)/shard_map/ppermute | solution.py:20
  134.9 5.6 %collective-permute-done.1 = bf16[2,2,2,64,2560]{4,3,2,1,0:T(8,128)(2,1)} collective-permute-done((bf16[2,2,2,64,2560]{4,3,2,1,0:T(8,128)(2,1)}, bf16[2,2,2,64,2560]{4,3,2,1,0:T(8,128)(2,1)}, u32[]{:S(2)}, u32[]{:S(2)}) %collective-permute-start.1) | collective-permute-done | bytes 2621472 | tf_op jit(solution)/shard_map/ppermute | solution.py:21
  140.6 3.5 %pad_maximum_fusion = bf16[2,2,6,64,2560]{4,3,2,1,0:T(8,128)(2,1)S(1)} fusion(bf16[2,2,2,64,2560]{4,3,2,1,0:T(8,128)(2,1)} %collective-permute-done.1, bf16[1,2,2,64,2560]{4,3,2,1,0:T(8,128)(2,1)S(1)} %bitcast.77, bf16[1,2,2,64,2560]{4,3,2,1,0:T(8,128)(2,1)S(1)} %bitcast.79, bf16[2,2,2,64,2560]{4,3,2,1,0:T(8,128)(2,1)} %collective-permute-done), kind=kLoop, calls=%fused_computation.23 | loop fusion | flops 11796480 | bytes 15728640 | tf_op jit(solution)/shard_map/concatenate | solution.py:22
  144.1 3.4 %fusion.32 = (bf16[1,2,6,64,2560]{4,3,2,1,0:T(8,128)(2,1)}, bf16[1,2,6,64,2560]{4,3,2,1,0:T(8,128)(2,1)}) fusion(bf16[2,2,6,64,2560]{4,3,2,1,0:T(8,128)(2,1)S(1)} %pad_maximum_fusion), kind=kLoop, calls=%fused_computation.52 | loop fusion | bytes 15728640 | tf_op jit(solution)/shard_map/slice | solution.py:106
  147.6 2.1 collective-permute-start.6
  149.7 1.7 bitcast_dynamic-update-slice_fusion.4
  151.4 6.3 %copy.18 = bf16[768,2560]{0,1:T(8,128)(2,1)} copy(bf16[768,2560]{1,0:T(8,128)(2,1)} %bitcast.72) | data formatting | bytes 7864320 | tf_op jit(solution)/shard_map/reshape;squeeze | solution.py:106
  157.7 3.4 %bitcast_dynamic-update-slice_fusion.3 = bf16[5,2,2,2,64,2560]{5,4,3,2,1,0:T(8,128)(2,1)} fusion(bf16[5,2,2,2,64,2560]{5,4,3,2,1,0:T(8,128)(2,1)} %bitcast_dynamic-update-slice_fusion.4, bf16[2,2,2,64,2560]{4,3,2,1,0:T(8,128)(2,1)} %collective-permute-done.3), kind=kLoop, calls=%fused_computation.31 | loop fusion | bytes 5242880
  161.1 3.4 %bitcast_dynamic-update-slice_fusion.2 = bf16[5,2,2,2,64,2560]{5,4,3,2,1,0:T(8,128)(2,1)} fusion(bf16[5,2,2,2,64,2560]{5,4,3,2,1,0:T(8,128)(2,1)} %bitcast_dynamic-update-slice_fusion.3, bf16[2,2,2,64,2560]{4,3,2,1,0:T(8,128)(2,1)} %collective-permute-done.4), kind=kLoop, calls=%fused_computation.30 | loop fusion | bytes 5242880
  164.5 3.5 %bitcast_dynamic-update-slice_fusion.1 = bf16[5,2,2,2,64,2560]{5,4,3,2,1,0:T(8,128)(2,1)} fusion(bf16[5,2,2,2,64,2560]{5,4,3,2,1,0:T(8,128)(2,1)} %bitcast_dynamic-update-slice_fusion.2, bf16[2,2,2,64,2560]{4,3,2,1,0:T(8,128)(2,1)} %collective-permute-done.5), kind=kLoop, calls=%fused_computation.29 | loop fusion | bytes 5242880
  167.9 13.7 %collective-permute-done.6 = bf16[2,2,2,64,2560]{4,3,2,1,0:T(8,128)(2,1)S(1)} collective-permute-done((bf16[2,2,2,64,2560]{4,3,2,1,0:T(8,128)(2,1)}, bf16[2,2,2,64,2560]{4,3,2,1,0:T(8,128)(2,1)S(1)}, u32[]{:S(2)}, u32[]{:S(2)}) %collective-permute-start.6) | collective-permute-done | bytes 2621472 | tf_op jit(solution)/shard_map/ppermute | solution.py:29
  181.6 1.8 bitcast_dynamic-update-slice_fusion
  183.4 9.8 %fusion.31 = (bf16[5,2,2,2,64,1280]{5,4,3,2,1,0:T(8,128)(2,1)}, bf16[5,2,2,2,64,1280]{5,4,3,2,1,0:T(8,128)(2,1)}) fusion(bf16[5,2,2,2,64,2560]{5,4,3,2,1,0:T(8,128)(2,1)} %bitcast_dynamic-update-slice_fusion), kind=kLoop, calls=%fused_computation.51 | loop fusion | bytes 26214400 | tf_op jit(solution)/shard_map/jit(_take)/gather | solution.py:88
  193.2 5.8 %gather_fusion = bf16[3,2,2,2,64,1280]{5,4,3,2,1,0:T(8,128)(2,1)} fusion(bf16[5,2,2,2,64,1280]{5,4,3,2,1,0:T(8,128)(2,1)} %get-tuple-element.71, s32[1024]{0:T(1024)S(1)} %pad_clamp_fusion), kind=kCustom, calls=%fused_computation | custom fusion | bytes 7864332 | tf_op jit(solution)/shard_map/jit(_take)/gather | solution.py:88
  199.0 5.7 %gather_fusion.1 = bf16[3,2,2,2,64,1280]{5,4,3,2,1,0:T(8,128)(2,1)} fusion(bf16[5,2,2,2,64,1280]{5,4,3,2,1,0:T(8,128)(2,1)} %get-tuple-element.72, s32[1024]{0:T(1024)S(1)} %pad_clamp_fusion), kind=kCustom, calls=%fused_computation.1 | custom fusion | bytes 7864332 | tf_op jit(solution)/shard_map/jit(_take)/gather | solution.py:88
  204.7 8.3 %maximum_select_fusion = bf16[3,2,2,2,64,2560]{5,4,3,2,1,0:T(8,128)(2,1)} fusion(bf16[3,2,2,2,64,1280]{5,4,3,2,1,0:T(8,128)(2,1)} %gather_fusion.1, bf16[3,2,2,2,64,1280]{5,4,3,2,1,0:T(8,128)(2,1)} %gather_fusion, pred[3]{0:T(512)(128)(4,1)S(1)} %compare_and_fusion.1), kind=kLoop, calls=%fused_computation.24 | loop fusion | flops 19660800 | bytes 15728643 | tf_op jit(solution)/shard_map/jit(_take)/select_n | solution.py:88
  212.9 5.4 %fusion.33 = (bf16[3,1,2,2,64,2560]{5,4,3,2,1,0:T(8,128)(2,1)}, bf16[3,1,2,2,64,2560]{5,4,3,2,1,0:T(8,128)(2,1)}) fusion(bf16[3,2,2,2,64,2560]{5,4,3,2,1,0:T(8,128)(2,1)} %maximum_select_fusion), kind=kLoop, calls=%fused_computation.53 | loop fusion | bytes 15728640 | tf_op jit(solution)/shard_map/slice | solution.py:106
  218.4 6.2 %copy.19 = bf16[768,2560]{0,1:T(8,128)(2,1)} copy(bf16[768,2560]{1,0:T(8,128)(2,1)} %bitcast.73) | data formatting | bytes 7864320 | tf_op jit(solution)/shard_map/reshape;squeeze | solution.py:106
  224.5 6.9 %pad_maximum_fusion.2 = bf16[1536,2560]{0,1:T(8,128)(2,1)} fusion(bf16[768,2560]{0,1:T(8,128)(2,1)} %copy.19, bf16[768,2560]{0,1:T(8,128)(2,1)} %copy.18), kind=kLoop, calls=%fused_computation.26 | loop fusion | flops 15728640 | bytes 15728640 | tf_op jit(solution)/shard_map/concatenate | solution.py:105
  231.5 7.0 %pad_maximum_fusion.1 = bf16[1536,2560]{1,0:T(8,128)(2,1)} fusion(bf16[768,2560]{1,0:T(8,128)(2,1)} %bitcast.75, bf16[768,2560]{1,0:T(8,128)(2,1)} %bitcast.74), kind=kLoop, calls=%fused_computation.25 | loop fusion | flops 15728640 | bytes 15728640 | tf_op jit(solution)/shard_map/concatenate | solution.py:108
  238.4 88.9 %while.10 = (s32[]{:T(128)}, bf16[10,256,256]{1,2,0:T(8,128)(2,1)}, s32[10]{0:T(128)S(1)}, bf16[1536,2560]{1,0:T(8,128)(2,1)}, pred[256,1536]{1,0:T(8,128)(4,1)S...) while((s32[]{:T(128)}, bf16[10,256,256]{1,2,0:T(8,128)(2,1)}, ...), condition=%wide.region_3.4_spmd, body=%wide.region_0.0_spmd.sunk | while | flops 611978752 | bytes 9048755 | solution.py:66
  327.3 3.5 %copy.22 = bf16[256,10,256]{2,1,0:T(8,128)(2,1)S(1)} copy(bf16[256,10,256]{0,2,1:T(8,128)(2,1)} %bitcast.83) | data formatting | bytes 2621440 | tf_op jit(solution)/shard_map/transpose | solution.py:67
  330.8 1.7 reshape_reshape.3
  (119 shorter events, 85.7 us)
Async XLA Ops:
  0.0 140.6 %copy-start.1 = (bf16[2,2,64,2560]{3,2,1,0:T(8,128)(2,1)S(1)}, bf16[2,2,64,2560]{3,2,1,0:T(8,128)(2,1)}, u32[]{:S(2)}) copy-start(bf16[2,2,64,2560]{3,2,1,0:T(8,128)(2,1)} %param.8) | copy-start | bytes 3932164
  0.0 140.6 %copy-start = (bf16[2,2,64,2560]{3,2,1,0:T(8,128)(2,1)S(1)}, bf16[2,2,64,2560]{3,2,1,0:T(8,128)(2,1)}, u32[]{:S(2)}) copy-start(bf16[2,2,64,2560]{3,2,1,0:T(8,128)(2,1)} %param.9) | copy-start | bytes 3932164
  0.0 82.0 %copy-start.4 = (s32[1,1,3]{2,1,0:T(1,128)S(1)}, s32[1,1,3]{2,1,0:T(1,128)}, u32[]{:S(2)}) copy-start(s32[1,1,3]{2,1,0:T(1,128)} %param.10) | copy-start | bytes 40
  3.6 34.1 %collective-permute-start.2 = (bf16[2,2,2,64,2560]{4,3,2,1,0:T(8,128)(2,1)}, bf16[2,2,2,64,2560]{4,3,2,1,0:T(8,128)(2,1)S(1)}, u32[]{:S(2)}, u32[]{:S(2)}) collective-permute-start(bf16[2,2,2,64,2560]{4,3,2,1,0:T(8,128)(2,1)} %pad_maximum_fusion.3), channel_id=1, source_target_pairs={{0,2},{2,4},{4,6},{6,8},{8,10},{10,12},{12,14},{14,16},{16,18},{18... | collective-permute-start | bytes 7864328 | tf_op jit(solution)/shard_map/ppermute | solution.py:29
  37.7 1.5 copy-start.2
  39.2 34.0 %collective-permute-start.3 = (bf16[2,2,2,64,2560]{4,3,2,1,0:T(8,128)(2,1)S(1)}, bf16[2,2,2,64,2560]{4,3,2,1,0:T(8,128)(2,1)}, u32[]{:S(2)}, u32[]{:S(2)}) collective-permute-start(bf16[2,2,2,64,2560]{4,3,2,1,0:T(8,128)(2,1)S(1)} %collective-permute-done.2), channel_id=1, source_target_pairs={{0,2},{2,4},{4,6},{6,8},{8,10},{10,12},{12,14},{14,16},{16,18},{18... | collective-permute-start | bytes 7864328 | tf_op jit(solution)/shard_map/ppermute | solution.py:29
  73.2 34.2 %collective-permute-start.4 = (bf16[2,2,2,64,2560]{4,3,2,1,0:T(8,128)(2,1)}, bf16[2,2,2,64,2560]{4,3,2,1,0:T(8,128)(2,1)}, u32[]{:S(2)}, u32[]{:S(2)}) collective-permute-start(bf16[2,2,2,64,2560]{4,3,2,1,0:T(8,128)(2,1)} %collective-permute-done.3), channel_id=1, source_target_pairs={{0,2},{2,4},{4,6},{6,8},{8,10},{10,12},{12,14},{14,16},{16,18},{18... | collective-permute-start | bytes 7864328 | tf_op jit(solution)/shard_map/ppermute | solution.py:29
  75.1 59.8 %collective-permute-start = (bf16[2,2,2,64,2560]{4,3,2,1,0:T(8,128)(2,1)}, bf16[2,2,2,64,2560]{4,3,2,1,0:T(8,128)(2,1)}, u32[]{:S(2)}, u32[]{:S(2)}) collective-permute-start(bf16[2,2,2,64,2560]{4,3,2,1,0:T(8,128)(2,1)} %pad_maximum_fusion.3), channel_id=1, source_target_pairs={{0,1},{2,3},{4,5},{6,7},{8,9},{10,11},{12,13},{14,15},{16,17},{18,... | collective-permute-start | bytes 7864328 | tf_op jit(solution)/shard_map/ppermute | solution.py:20
  80.1 60.5 %collective-permute-start.1 = (bf16[2,2,2,64,2560]{4,3,2,1,0:T(8,128)(2,1)}, bf16[2,2,2,64,2560]{4,3,2,1,0:T(8,128)(2,1)}, u32[]{:S(2)}, u32[]{:S(2)}) collective-permute-start(bf16[2,2,2,64,2560]{4,3,2,1,0:T(8,128)(2,1)} %pad_maximum_fusion.3), channel_id=1, source_target_pairs={{1,0},{3,2},{5,4},{7,6},{9,8},{11,10},{13,12},{15,14},{17,16},{19,... | collective-permute-start | bytes 7864328 | tf_op jit(solution)/shard_map/ppermute | solution.py:21
  107.4 40.2 %collective-permute-start.5 = (bf16[2,2,2,64,2560]{4,3,2,1,0:T(8,128)(2,1)}, bf16[2,2,2,64,2560]{4,3,2,1,0:T(8,128)(2,1)}, u32[]{:S(2)}, u32[]{:S(2)}) collective-permute-start(bf16[2,2,2,64,2560]{4,3,2,1,0:T(8,128)(2,1)} %collective-permute-done.4), channel_id=1, source_target_pairs={{0,2},{2,4},{4,6},{6,8},{8,10},{10,12},{12,14},{14,16},{16,18},{18... | collective-permute-start | bytes 7864328 | tf_op jit(solution)/shard_map/ppermute | solution.py:29
  144.1 5.6 %copy-start.3 = (bf16[2,2,2,64,2560]{4,3,2,1,0:T(8,128)(2,1)S(1)}, bf16[2,2,2,64,2560]{4,3,2,1,0:T(8,128)(2,1)}, u32[]{:S(2)}) copy-start(bf16[2,2,2,64,2560]{4,3,2,1,0:T(8,128)(2,1)} %copy-done.2) | copy-start | bytes 7864324
  147.6 34.1 %collective-permute-start.6 = (bf16[2,2,2,64,2560]{4,3,2,1,0:T(8,128)(2,1)}, bf16[2,2,2,64,2560]{4,3,2,1,0:T(8,128)(2,1)S(1)}, u32[]{:S(2)}, u32[]{:S(2)}) collective-permute-start(bf16[2,2,2,64,2560]{4,3,2,1,0:T(8,128)(2,1)} %collective-permute-done.5), channel_id=1, source_target_pairs={{0,2},{2,4},{4,6},{6,8},{8,10},{10,12},{12,14},{14,16},{16,18},{18... | collective-permute-start | bytes 7864328 | tf_op jit(solution)/shard_map/ppermute | solution.py:29
where the time goes:
time: 334 us; the launch traced here: 332 us
  waiting for transfers between devices  134 us (40%)
  local copies, waits for them, and re-layouts  113 us (34%)
  matrix products  32.6 us (10%)
  other arithmetic  29.7 us (9%)
  starting transfers between devices  16 us (5%)
  loops' own time  6.73 us (2%)
    ppermute x5, waiting for transfers between devices, from_behind(): lax.ppermute(value, axis, [(source, source + steps) for source in range(l...  103 us
    ppermute x1, waiting for transfers between devices, padded_2(): before = lax.ppermute(last, axis, up)  24.9 us
    gather x3, local copies, waits for them, and re-layouts, local(): chosen = jnp.take(stacked, position, axis=0)  21.2 us
    sub x10, matrix products, one_group(): weights = jnp.where(allowed[None], jnp.exp(scores - maximum), 0.0)  16.4 us
    dot_general x10, matrix products, one_group(): jnp.einsum('hqk,khd->qhd', weights.astype(jnp.bfloat16), value_part, pref...  16.3 us
    dynamic_slice x20, local copies, waits for them, and re-layouts, one_group(): lax.dynamic_slice_in_dim(value_rows, offset, columns, 1)  14.7 us
    unnamed x14, local copies, waits for them, and re-layouts  13.5 us
    dynamic_slice x10, local copies, waits for them, and re-layouts, one_group(): lax.dynamic_slice_in_dim(key_rows, offset, columns, 1)  11.9 us
  transfers between devices with their start and end apart: 7, of which 6 were waited for; matrix products, arithmetic and copies ran while one was open for 8% of the time, Pallas kernels for 0%

commit v1 on v0

v1 whole, which is shorter than its diff:
```python
import functools
import math

import jax
import jax.numpy as jnp
from jax import lax
from jax.experimental import pallas as pl
from jax.experimental.pallas import tpu as pltpu
from jax.sharding import PartitionSpec as P

HD = 128
HMAX = 2
WIN = 5
UP, DOWN = WIN + 1, WIN + 2
SLOTS = WIN + 3
AHEAD = 2
LOW = -1e30
SCALE = math.log2(math.e) / math.sqrt(HD)

ROUTES = (
    ((0, 0, 4, None), (0, 0, 2, None), (0, 0, 1, None), (1, 4, 5, None), (1, 2, 3, None)),
    (
        (0, 0, 2, None),
        (0, 0, 4, 0),
        (1, 2, 5, 1),
        (1, 4, 5, 0),
        (1, 2, 1, None),
        (1, 4, 3, 0),
        (2, 5, 3, 1),
        (3, 3, 4, 1),
    ),
    ((0, 0, 4, None), (0, 0, 1, None), (1, 4, 2, None), (1, 4, 5, None), (2, 2, 3, None)),
    ((0, 0, 4, None), (1, 4, 2, None), (1, 4, 3, None), (2, 2, 5, None), (2, 2, 1, None)),
)
GROUP = len(ROUTES)
STAGES = 4


def sends_of(role):
    found = []
    for origin, rows in enumerate(ROUTES):
        for stage, src, dst, parity in rows:
            if (origin + src) % GROUP == role:
                found.append((stage, src, dst - src, dst, parity))
    return found


MOST = max(len(sends_of(role)) for role in range(GROUP))


def both(*terms):
    out = terms[0]
    for term in terms[1:]:
        out = jnp.logical_and(out, term)
    return out


def kernel(count, tiles, shape, lists_ref, halo_ref, q_ref, k_ref, v_ref, out_ref,
           kv, q_v, bias, local_sem, q_sem, send_sem, recv_sem):
    frames, rows, columns = shape
    tokens = frames * rows * columns
    heads = q_ref.shape[1] // HD
    block = lax.axis_index("tm")
    tile = lax.axis_index("tile")
    role = block % GROUP

    def part(ref, head):
        return ref.at[:, pl.ds(pl.multiple_of(head * HD, HD), HD)]

    def fetch(head, carry):
        pltpu.make_async_copy(part(k_ref, head), kv.at[0, head, 0], local_sem.at[head]).start()
        pltpu.make_async_copy(part(v_ref, head), kv.at[0, head, 1], local_sem.at[head]).start()
        return carry

    lax.fori_loop(0, heads, fetch, 0)
    q_copy = pltpu.make_async_copy(q_ref, q_v, q_sem)
    q_copy.start()

    barrier = pltpu.get_barrier_semaphore()
    expected = jnp.int32(0)
    partners = [("tm", block, count, step) for step in range(-WIN, WIN + 1) if step]
    partners += [("tile", tile, tiles, step) for step in (-1, 1)]
    for axis, me, size, step in partners:
        there = both(me + step >= 0, me + step < size)

        @pl.when(there)
        def _():
            pl.semaphore_signal(barrier, inc=1, device_id={axis: me + step},
                                device_id_type=pl.DeviceIdType.MESH)

        expected += there.astype(jnp.int32)

    missing = [(d, block < d) for d in range(1, WIN + 1)]
    missing += [(UP, tile < 1), (DOWN, tile + 1 >= tiles)]
    for slot, gone in missing:

        @pl.when(gone)
        def _():
            def clear(head, carry):
                kv[slot, head] = jnp.zeros(kv.shape[2:], kv.dtype)
                return carry

            lax.fori_loop(0, heads, clear, 0)

    reach = halo_ref[0]
    query = lax.broadcasted_iota(jnp.int32, (tokens, tokens), 0) // (rows * columns)
    key = lax.broadcasted_iota(jnp.int32, (tokens, tokens), 1)
    key_row = (key // columns) % rows
    causal = key // (rows * columns) <= query
    above = both(causal, key_row >= rows - reach, tile >= 1)
    below = both(causal, key_row < reach, tile + 1 < tiles)
    for at, mask in enumerate((causal, above, below)):
        bias[at] = jnp.where(mask, 0.0, LOW)

    present = []
    for d in range(1, WIN + 1):
        hit = lists_ref[0] == block - d
        for n in range(1, lists_ref.shape[0]):
            hit = jnp.logical_or(hit, lists_ref[n] == block - d)
        present.append(jnp.logical_and(hit, block >= d))

    pl.semaphore_wait(barrier, expected)

    def remote(src, dst, head, sem, target):
        return pltpu.make_async_remote_copy(
            src_ref=kv.at[src, head],
            dst_ref=kv.at[dst, head],
            send_sem=send_sem.at[sem],
            recv_sem=recv_sem.at[dst, head],
            device_id=target,
            device_id_type=pl.DeviceIdType.MESH,
        )

    def arrived(slot, head):
        remote(slot, slot, head, 0, {"tm": block}).wait_recv()

    def own(head):
        pltpu.make_async_copy(kv.at[0, head], kv.at[0, head], local_sem.at[head]).wait()

        @pl.when(tile + 1 < tiles)
        def _():
            remote(0, UP, head, MOST, {"tile": tile + 1}).start()

        @pl.when(tile >= 1)
        def _():
            remote(0, DOWN, head, MOST + 1, {"tile": tile - 1}).start()

        relay(0, head)

    def relay(stage, head):
        for mine in range(GROUP):
            entries = [(at, *e) for at, e in enumerate(sends_of(mine)) if e[0] == stage]
            if not entries:
                continue

            @pl.when(role == mine)
            def _():
                for slot in sorted({e[2] for e in entries}):
                    group = [e for e in entries if e[2] == slot]
                    parities = {e[5] for e in group}
                    if slot:
                        needed = block >= slot
                        if None not in parities:
                            needed = both(needed, head % 2 == min(parities))

                        @pl.when(needed)
                        def _():
                            arrived(slot, head)

                    for at, _, _, step, dst, parity in group:
                        go = both(block >= slot, block + step < count)
                        if parity is not None:
                            go = both(go, head % 2 == parity)

                        @pl.when(go)
                        def _():
                            remote(slot, dst, head, at, {"tm": block + step}).start()

    def leaves(head):
        for mine in range(GROUP):
            entries = sends_of(mine)

            @pl.when(role == mine)
            def _():
                for slot in range(1, WIN + 1):
                    parities = {e[4] for e in entries if e[1] == slot}
                    if None in parities or parities == {0, 1}:
                        continue
                    needed = block >= slot
                    if parities:
                        needed = both(needed, head % 2 != min(parities))

                    @pl.when(needed)
                    def _():
                        arrived(slot, head)

        @pl.when(tile >= 1)
        def _():
            arrived(UP, head)

        @pl.when(tile + 1 < tiles)
        def _():
            arrived(DOWN, head)

    def attend(head):
        query_part = part(q_v, head)[...]
        scores = []
        tops = []
        for slot in range(SLOTS):
            s = lax.dot_general(query_part, kv[slot, head, 0], (((1,), (1,)), ((), ())),
                                preferred_element_type=jnp.float32)
            if slot == 0:
                s = s + bias[0]
            elif slot > WIN:
                s = s + bias[slot - WIN]
            top = jnp.max(s, axis=1, keepdims=True)
            if 0 < slot <= WIN:
                top = jnp.where(present[slot - 1], top, LOW)
            scores.append(s)
            tops.append(top)
        top = functools.reduce(jnp.maximum, tops) * SCALE
        total = None
        numerator = None
        for slot in range(SLOTS):
            shift = jnp.where(present[slot - 1], top, -LOW) if 0 < slot <= WIN else top
            w = jnp.exp2(scores[slot] * SCALE - shift)
            total = w if total is None else total + w
            term = jnp.dot(w.astype(jnp.bfloat16), kv[slot, head, 1],
                           preferred_element_type=jnp.float32)
            numerator = term if numerator is None else numerator + term
        total = jnp.sum(total, axis=1, keepdims=True)
        part(out_ref, head)[...] = (numerator / total).astype(out_ref.dtype)

    def first(head, carry):
        own(head)
        return carry

    lax.fori_loop(0, AHEAD, first, 0)
    q_copy.wait()

    def step(t, carry):
        @pl.when(t + AHEAD < heads)
        def _():
            own(t + AHEAD)

        for stage in range(1, STAGES):
            head = t - (stage - 1)

            @pl.when(both(head >= 0, head < heads))
            def _():
                relay(stage, head)

        head = t - (STAGES - 1)

        @pl.when(head >= 0)
        def _():
            leaves(head)
            attend(head)

        return carry

    lax.fori_loop(0, heads + STAGES - 1, step, 0)

    def sent(slot, parity, sem):
        size = heads if parity is None else (heads + 1 - parity) // 2
        ref = kv.at[slot, pl.ds(0, size)]
        pltpu.make_async_remote_copy(
            src_ref=ref, dst_ref=ref, send_sem=send_sem.at[sem], recv_sem=recv_sem.at[0, 0],
            device_id={"tm": block}, device_id_type=pl.DeviceIdType.MESH,
        ).wait_send()

    for mine in range(GROUP):

        @pl.when(role == mine)
        def _():
            for at, (_, slot, step_, dst, parity) in enumerate(sends_of(mine)):

                @pl.when(both(block >= slot, block + step_ < count))
                def _():
                    sent(slot, parity, at)

    @pl.when(tile + 1 < tiles)
    def _():
        sent(0, None, MOST)

    @pl.when(tile >= 1)
    def _():
        sent(0, None, MOST + 1)


def local(count, tiles, queries, keys, values, neighbours, halo_rows):
    frames, rows, columns, channels = queries.shape
    tokens = frames * rows * columns
    heads = channels // HD
    assert rows == HMAX and count % GROUP == 0
    flat = (tokens, channels)
    smem = pl.BlockSpec(memory_space=pltpu.SMEM)
    anywhere = pl.BlockSpec(memory_space=pl.ANY)
    out = pl.pallas_call(
        functools.partial(kernel, count, tiles, (frames, rows, columns)),
        out_shape=jax.ShapeDtypeStruct(flat, jnp.bfloat16),
        in_specs=[smem, smem, anywhere, anywhere, anywhere],
        out_specs=pl.BlockSpec(memory_space=pltpu.VMEM),
        scratch_shapes=[
            pltpu.VMEM((SLOTS, heads, 2, tokens, HD), jnp.bfloat16),
            pltpu.VMEM(flat, jnp.bfloat16),
            pltpu.VMEM((3, tokens, tokens), jnp.float32),
            pltpu.SemaphoreType.DMA((heads,)),
            pltpu.SemaphoreType.DMA,
            pltpu.SemaphoreType.DMA((MOST + 2,)),
            pltpu.SemaphoreType.DMA((SLOTS, heads)),
        ],
        compiler_params=pltpu.CompilerParams(
            collective_id=0, has_side_effects=True, vmem_limit_bytes=56 * 1024 * 1024
        ),
    )(
        neighbours.reshape(-1),
        halo_rows.reshape(-1),
        queries.reshape(flat),
        keys.reshape(flat),
        values.reshape(flat),
    )
    return out.reshape(queries.shape)


def solution(mesh):
    return jax.shard_map(
        functools.partial(local, mesh.shape["tm"], mesh.shape["tile"]),
        mesh=mesh,
        in_specs=(
            P("tm", "tile", None, None),
            P("tm", "tile", None, None),
            P("tm", "tile", None, None),
            P("tm", "tile", None),
            P("tm", "tile"),
        ),
        out_specs=P("tm", "tile", None, None),
        check_vma=False,
    )
```

time: 334 us -> 97.9 us (0.29)
  waiting for transfers between devices: 134 us -> 0 us
  local copies, waits for them, and re-layouts: 113 us -> 2.46 us
  Pallas kernels: 0 us -> 92.9 us
  matrix products: 32.6 us -> 0 us
  other arithmetic: 29.7 us -> 0 us
  starting transfers between devices: 16 us -> 0 us
  loops' own time: 6.73 us -> 0 us
    ppermute x7 -> x0, waiting for transfers between devices: 134 us -> none  [the longest x5 103 us: from_behind(): lax.ppermute(value, axis, [(source, source + steps) for source in range(l...]
    pallas_call x0 -> x1, Pallas kernels: none -> 92.9 us  [local(): pl.pallas_call(functools.partial(kernel, count, tiles, (frames, rows, col...]
    dynamic_slice x60 -> x0, local copies, waits for them, and re-layouts: 42.8 us -> none  [the longest x20 14.7 us: one_group(): lax.dynamic_slice_in_dim(value_rows, offset, columns, 1)]
    gather x3 -> x0, local copies, waits for them, and re-layouts: 21.2 us -> none  [local(): chosen = jnp.take(stacked, position, axis=0)]
    concatenate x4 -> x0, other arithmetic: 17.6 us -> none  [the longest x1 6.97 us: local(): jnp.concatenate((padded[1].reshape(-1, channels), chosen[:, 1].reshape(-1...]
    sub x10 -> x0, matrix products: 16.4 us -> none  [one_group(): weights = jnp.where(allowed[None], jnp.exp(scores - maximum), 0.0)]
    dot_general x10 -> x0, matrix products: 16.3 us -> none  [one_group(): jnp.einsum('hqk,khd->qhd', weights.astype(jnp.bfloat16), value_part, pref...]
    ppermute x7 -> x0, starting transfers between devices: 16 us -> none  [the longest x5 9.73 us: from_behind(): lax.ppermute(value, axis, [(source, source + steps) for source in range(l...]
  transfers between devices with their start and end apart: 7 -> 0, of which waited for: 6 -> 0; matrix products, arithmetic and copies ran while one was open for 8% -> 0% of each run, Pallas kernels for 0% -> 0%
where the time goes in v1:
time: 97.9 us; the launch traced here: 96.1 us
  Pallas kernels  92.9 us (95%)
  local copies, waits for them, and re-layouts  2.46 us (3%)
    pallas_call x1, Pallas kernels, local(): pl.pallas_call(functools.partial(kernel, count, tiles, (frames, rows, col...  92.9 us
    unnamed x1, local copies, waits for them, and re-layouts  2.46 us

profile of v1, /device:TPU:16, one launch (start us, length us, event | category | flops | bytes accessed | tf_op | source)
XLA Modules:
  0.0 96.1 jit_solution(147547011229466658)
XLA Ops:
  0.7 92.9 %shard_map.55 = bf16[256,2560]{1,0:T(8,128)(2,1)} custom-call(s32[3]{0:T(128)} %bitcast.11, s32[1]{0:T(128)} %bitcast.6.halo_ref, bf16[256,2560]{1,0:T(8,128)(2,1)} %bitcast.8, bf16[256,2560]{1,0:T(8,128)(2,1)} %bitcast.9, bf16[256,2560]{1,0:T(8,128)(2,1)} %bitcast.10), custom_call_target="tpu_custom_call" | custom-call | tf_op jit(solution)/shard_map/pallas_call | solution.py:299
  93.6 2.5 %copy.8 = bf16[2,2,64,2560]{3,2,1,0:T(8,128)(2,1)} copy(bf16[2,2,64,2560]{3,2,1,0:T(8,128)(2,1)} %bitcast.7) | data formatting | bytes 2621440
